TPU v7x, 128 devices: a whole 4x4x4 slice. The times are simulated.
128 devices in a mesh: rows: 16 (over x, y_lo, core), dim: 8 (over y_hi, z).
Axes of the slice: x: 4, y: 4 (y_hi: 2, y_lo: 2; y = y_hi * 2 + y_lo), z: 4, core: 2. Of those that a mesh axis runs over, the one named last changes fastest.
Arguments:
- entity_table: float32 [524288, 512], P(('rows', 'dim')), may hold values from -2.5 to 2.5
- relations: float32 [822, 512], replicated, may hold values from -6 to 6
- thresholds: float32 [64], replicated, may hold values from 0.2 to 2
- head_ids: int32 [2048], replicated, may hold values from 0 to 524287
- rel_ids: int32 [2048], replicated, may hold values from 0 to 821
- thr_idx: int32 [2048], replicated, may hold values from 0 to 63
Outputs:
- serving_table: float32 [524288, 512], P('rows', 'dim')
- fraction: float32 [2048], P(('rows', 'dim'))
All inputs are finite; a program needn't handle non-finite values.
Results may differ from a plain program's by a relative error of at most 0.0011.
Values sent between devices are 32-bit elements; how exact they have to be, the bound alone decides.
No kernel may reach another device: no remote copies, remote signals or barrier semaphores. Data moves between devices by JAX's collectives and lax.ppermute only.
A program may use at most 128 MiB of HBM per device.

v0:
```python
import jax
import jax.numpy as jnp
from jax import lax
from jax.sharding import PartitionSpec as P

sharpness = 2.0


def cut_along(value, dim, length):
    lengths = value.shape
    parts = value.reshape(*lengths[:dim], length, lengths[dim] // length, *lengths[dim + 1 :])
    return jnp.moveaxis(parts, dim, 0)


def cut_rows(length, count):
    lap = length // count
    if lap >= 8:
        lap -= lap % 8
    return [lap * k for k in range(1, count)]


def joined_along(parts, dim):
    lengths = list(parts.shape[1:])
    lengths[dim] *= parts.shape[0]
    return jnp.moveaxis(parts, 0, dim).reshape(lengths)


def several_exchanges(value, axis, pieces, split_dim, concat_dim):
    parts = cut_along(value, split_dim, lax.axis_size(axis))
    cut = max(range(1, max(2, parts.ndim - 1)), key=lambda d: parts.shape[d])
    outs = []
    for slab in jnp.split(parts, cut_rows(parts.shape[cut], pieces), axis=cut):
        if slab.size:
            outs.append(lax.all_to_all(slab, axis, split_axis=0, concat_axis=0, tiled=True))
    return joined_along(jnp.concatenate(outs, axis=cut), concat_dim)


def pick_rows(table, head_ids, start):
    count = table.shape[0]
    local = head_ids - start
    owned = (local >= 0) & (local < count)
    picked = jnp.take(table, jnp.clip(local, 0, count - 1), axis=0)
    return jnp.where(owned[:, None], picked, jnp.zeros_like(picked))


def shards(entity_table, relations, thresholds, head_ids, rel_ids, thr_idx):
    local_rows = entity_table.shape[0]
    width = entity_table.shape[1]
    total_ents = local_rows * lax.axis_size("rows") * lax.axis_size("dim")
    serving = several_exchanges(entity_table, "dim", 2, 1, 0)
    start = (lax.axis_index("rows") * lax.axis_size("dim") + lax.axis_index("dim")) * local_rows
    partial_value = pick_rows(entity_table, head_ids, start)
    head_vecs = lax.psum(partial_value, ("rows", "dim"))
    query = (head_vecs * jnp.take(relations, rel_ids, axis=0)).astype(jnp.bfloat16)
    ent_low = entity_table.astype(jnp.bfloat16)
    level = jnp.take(thresholds, thr_idx)
    queries = query.shape[0]
    query_blocks = query.reshape(queries // 512, 512, width)
    level_blocks = level.reshape(queries // 512, 512)

    def score_block(pair):
        rows_q, rows_level = pair
        score = jnp.dot(rows_q, ent_low.T, preferred_element_type=jnp.float32)
        soft = jax.nn.sigmoid(sharpness * (score - rows_level[:, None]))
        return jnp.sum(soft, axis=1) * (1.0 / total_ents)

    partial_share = lax.map(score_block, (query_blocks, level_blocks)).reshape(queries)
    fraction = lax.psum_scatter(partial_share, ("rows", "dim"), scatter_dimension=0, tiled=True)
    return (serving, fraction)


def solution(mesh):
    placed = (P(("rows", "dim"), None), P(), P(), P(), P(), P())
    return jax.shard_map(
        shards,
        mesh=mesh,
        in_specs=placed,
        out_specs=(P("rows", "dim"), P(("rows", "dim"))),
        check_vma=False,
    )
```

profile of v0, /device:TPU:1, one launch (start us, length us, event | category | flops | bytes accessed | tf_op | source)
XLA Modules:
  0.0 349.4 jit_solution(9521090022698641144)
XLA Ops:
  7.2 0.0 copy-start
  7.2 9.0 %copy.12 = f32[4096,512]{0,1:T(8,128)} copy(f32[4096,512]{1,0:T(8,128)} %param.8) | data formatting | bytes 16777216 | tf_op args[0]
  16.2 7.9 %fusion.6 = (f32[8,2048,64]{1,2,0:T(8,128)}, f32[8,2048,64]{1,2,0:T(8,128)}) fusion(f32[8,4096,64]{1,2,0:T(8,128)} %bitcast.87), kind=kLoop, calls=%fused_computation.21 | loop fusion | bytes 16777216 | tf_op jit(solution)/shard_map/split | solution.py:32
  24.1 8.6 %all-to-all-start = ((f32[8,2048,64]{1,2,0:T(8,128)}), f32[8,2048,64]{1,2,0:T(8,128)}, u32[]{:S(2)}, u32[]{:S(2)}) async-start(f32[8,2048,64]{1,2,0:T(8,128)} %get-tuple-element.40), calls=%async_computation | async-start | bytes 8388608 | tf_op jit(solution)/shard_map/all_to_all | solution.py:34
  32.7 0.0 all-reduce.3.cloned.1.call-start
  32.8 12.9 %gather_fusion = f32[2048,512]{1,0:T(8,128)} fusion(f32[4096,512]{1,0:T(8,128)} %param.8, s32[2048]{0:T(1024)S(1)} %fusion.5), kind=kCustom, calls=%fused_computation | custom fusion | bytes 8396800 | tf_op jit(solution)/shard_map/jit(_take)/gather | solution.py:42
  45.7 4.0 %select_select_fusion = f32[2048,512]{1,0:T(8,128)} fusion(f32[2048,512]{1,0:T(8,128)} %gather_fusion, pred[2048]{0:T(1024)(128)(4,1)S(1)} %get-tuple-element.43, pred[2048]{0:T(1024)(128)(4,1)S(1)} %get-tuple-element.42), kind=kLoop, calls=%fused_computation.11 | loop fusion | flops 2097152 | bytes 8392704 | tf_op jit(solution)/shard_map/jit(_where)/select_n | solution.py:43
  49.6 0.0 all-reduce.3.cloned.1.call-update
  49.7 0.0 copy-start.2
  49.7 5.9 %convert_element_type.7 = bf16[4096,512]{1,0:T(8,128)(2,1)} convert(f32[4096,512]{1,0:T(8,128)} %param.8) | non-fusion elementwise | flops 2097152 | bytes 12582912 | tf_op jit(solution)/shard_map/convert_element_type | solution.py:55
  55.5 0.7 fusion.10
  56.2 0.7 fusion.8
  57.0 0.7 fusion.7
  57.7 0.7 fusion.9
  58.4 39.7 %select_select_fusion.1 = f32[2048]{0:T(1024)S(1)} fusion(s32[2048]{0:T(1024)S(1)} %copy-done.5, f32[]{:T(128)} %bitcast.7, f32[]{:T(128)} %bitcast.8, f32[]{:T(128)} %bitcast.9, f32[]{:T(128)} %bitcast.10, f32[]{:T(128)} %bitcast.11, f32[]{:T(128)} %bitcast.12, f32[]{:T(128)} %bitcast.13, f32[]{:T(128)} %bitcast.14, f32[]{:T(128)} %bitcast.15, f32[]{:T(128)} %bitcast.16, ...), kind=kLoop, calls=%fused_computation.15 | loop fusion | flops 272384 | bytes 16640 | tf_op jit(solution)/shard_map/jit(_take)/select_n | solution.py:56
  98.2 8.9 %gather_fusion.1 = f32[2048,512]{1,0:T(8,128)} fusion(f32[822,512]{1,0:T(8,128)S(1)} %copy-done, s32[2048]{0:T(1024)S(1)} %fusion.4), kind=kCustom, calls=%fused_computation.1 | custom fusion | bytes 8396800 | tf_op jit(solution)/shard_map/jit(_take)/gather | solution.py:54
  107.1 112.8 %all-reduce.3.cloned.1.call-done = f32[2048,512]{1,0:T(8,128)} async-done(((f32[2048,512]{1,0:T(8,128)}), f32[2048,512]{1,0:T(8,128)}) %all-reduce.3.cloned.1.call-update) | async-done | bytes 4194320 | tf_op jit(solution)/shard_map/psum | solution.py:53
  219.9 4.7 %multiply_convert_fusion = bf16[2048,512]{1,0:T(8,128)(2,1)} fusion(f32[2048,512]{1,0:T(8,128)} %all-reduce.3.cloned.1.call-done, f32[2048,512]{1,0:T(8,128)} %gather_fusion.1, pred[2048]{0:T(1024)(128)(4,1)S(1)} %compare_and_fusion), kind=kLoop, calls=%fused_computation.10 | loop fusion | flops 3145728 | bytes 10487808 | tf_op jit(solution)/shard_map/convert_element_type | solution.py:54
  224.6 4.7 %all-to-all-start.1 = ((f32[8,2048,64]{1,2,0:T(8,128)}), f32[8,2048,64]{1,2,0:T(8,128)}, u32[]{:S(2)}, u32[]{:S(2)}) async-start(f32[8,2048,64]{1,2,0:T(8,128)} %get-tuple-element.41), calls=%async_computation.1 | async-start | bytes 8388608 | tf_op jit(solution)/shard_map/all_to_all | solution.py:34
  229.4 22.9 %while.10 = (s32[]{:T(128)}, f32[4,512]{1,0:T(4,128)S(1)}, bf16[4,512,512]{2,1,0:T(8,128)(2,1)}, bf16[4096,512]{1,0:T(8,128)(2,1)}, f32[4,512]{1,0:T(4,128)S(1)}, /*index=5*/s32[]{:T(128)}, s32[]{:T(128)}) while((s32[]{:T(128)}, f32[4,512]{1,0:T(4,128)S(1)}, bf16[4,512,512]{2,1,0:T(8,128)(2,1)}, bf16[4096,512]{1,0:T(8,128)(2,1)}, ...), condition=%wide.region_3.4_spmd, body=%wide.region_1.3_spmd.sunk | while | flops 2160066560 | bytes 4735073 | solution.py:67
  229.4 5.6 %fusion.17 = f32[512]{0:T(512)S(1)} fusion(bf16[4096,512]{1,0:T(8,128)(2,1)} %get-tuple-element.156, f32[512]{0:T(512)S(1)} %bitcast.91, bf16[4,512,512]{2,1,0:T(8,128)(2,1)} %get-tuple-element.155, s32[]{:T(128)S(6)} %copy.20), kind=kOutput, calls=%fused_computation.3.clone.1 | convolution fusion | flops 2160066048 | bytes 4722692 | tf_op jit(solution)/shard_map/while/body/eval_jaxpr/dot_general | solution.py:63
  235.1 0.1 dynamic_update_slice.5
  235.1 5.6 %fusion.17 = f32[512]{0:T(512)S(1)} fusion(bf16[4096,512]{1,0:T(8,128)(2,1)} %get-tuple-element.156, f32[512]{0:T(512)S(1)} %bitcast.91, bf16[4,512,512]{2,1,0:T(8,128)(2,1)} %get-tuple-element.155, s32[]{:T(128)S(6)} %copy.20), kind=kOutput, calls=%fused_computation.3.clone.1 | convolution fusion | flops 2160066048 | bytes 4722692 | tf_op jit(solution)/shard_map/while/body/eval_jaxpr/dot_general | solution.py:63
  240.8 0.1 dynamic_update_slice.5
  240.9 5.6 %fusion.17 = f32[512]{0:T(512)S(1)} fusion(bf16[4096,512]{1,0:T(8,128)(2,1)} %get-tuple-element.156, f32[512]{0:T(512)S(1)} %bitcast.91, bf16[4,512,512]{2,1,0:T(8,128)(2,1)} %get-tuple-element.155, s32[]{:T(128)S(6)} %copy.20), kind=kOutput, calls=%fused_computation.3.clone.1 | convolution fusion | flops 2160066048 | bytes 4722692 | tf_op jit(solution)/shard_map/while/body/eval_jaxpr/dot_general | solution.py:63
  246.5 0.1 dynamic_update_slice.5
  246.6 5.6 %fusion.17 = f32[512]{0:T(512)S(1)} fusion(bf16[4096,512]{1,0:T(8,128)(2,1)} %get-tuple-element.156, f32[512]{0:T(512)S(1)} %bitcast.91, bf16[4,512,512]{2,1,0:T(8,128)(2,1)} %get-tuple-element.155, s32[]{:T(128)S(6)} %copy.20), kind=kOutput, calls=%fused_computation.3.clone.1 | convolution fusion | flops 2160066048 | bytes 4722692 | tf_op jit(solution)/shard_map/while/body/eval_jaxpr/dot_general | solution.py:63
  252.3 0.1 dynamic_update_slice.5
  252.4 81.6 %all-reduce = f32[2048]{0:T(1024)S(1)} all-reduce(f32[2048]{0:T(1024)S(1)} %bitcast.92), channel_id=2, replica_groups=mesh['rows'=16,'dim'=8] {'rows','dim'}, use_global_device_ids=true, to_apply=%region_4.5.clone | all-reduce | flops 2048 | bytes 16384
  334.0 0.6 dynamic-slice
  334.6 4.0 %maximum_bitcast_fusion = f32[8,8,8,4096]{3,2,1,0:T(8,128)S(1)} fusion(f32[8,2048,64]{1,2,0:T(8,128)} %all-to-all-done.1, f32[8,2048,64]{1,2,0:T(8,128)} %all-to-all-done), kind=kLoop, calls=%fused_computation.9 | loop fusion | flops 2097152 | bytes 16777216
  338.6 3.9 %copy.14 = f32[8,8,8,4096]{3,2,0,1:T(8,128)} copy(f32[8,8,8,4096]{3,2,1,0:T(8,128)S(1)} %maximum_bitcast_fusion) | data formatting | bytes 16777216 | tf_op jit(solution)/shard_map/reshape | solution.py:25
  (27 shorter events, 0.1 us)
Async XLA Ops:
  7.2 91.0 %copy-start = (f32[822,512]{1,0:T(8,128)S(1)}, f32[822,512]{1,0:T(8,128)}, u32[]{:S(2)}) copy-start(f32[822,512]{1,0:T(8,128)} %param.9) | copy-start | bytes 5050372
  24.1 8.7 %copy-start.4 = (s32[2048]{0:T(1024)S(1)}, s32[2048]{0:T(1024)}, u32[]{:S(2)}) copy-start(s32[2048]{0:T(1024)} %param.11) | copy-start | bytes 24580
  24.1 200.6 %all-to-all-start = ((f32[8,2048,64]{1,2,0:T(8,128)}), f32[8,2048,64]{1,2,0:T(8,128)}, u32[]{:S(2)}, u32[]{:S(2)}) async-start(f32[8,2048,64]{1,2,0:T(8,128)} %get-tuple-element.40), calls=%async_computation | async-start | bytes 8388608 | tf_op jit(solution)/shard_map/all_to_all | solution.py:34
  32.7 187.2 %all-reduce.3.cloned.1.call-start = ((), (), s32[]{:S(2)}) async-start(), calls=%async_computation.2 | async-start | bytes 8388608 | tf_op jit(solution)/shard_map/psum | solution.py:53
  49.7 5.9 %copy-start.2 = (f32[64]{0:T(128)S(1)}, f32[64]{0:T(128)}, u32[]{:S(2)}) copy-start(f32[64]{0:T(128)} %param.10) | copy-start | bytes 772
  49.7 8.7 %copy-start.5 = (s32[2048]{0:T(1024)S(1)}, s32[2048]{0:T(1024)}, u32[]{:S(2)}) copy-start(s32[2048]{0:T(1024)} %param.13) | copy-start | bytes 24580
  49.7 48.5 %copy-start.3 = (s32[2048]{0:T(1024)S(1)}, s32[2048]{0:T(1024)}, u32[]{:S(2)}) copy-start(s32[2048]{0:T(1024)} %param.12) | copy-start | bytes 24580
  224.6 109.9 %all-to-all-start.1 = ((f32[8,2048,64]{1,2,0:T(8,128)}), f32[8,2048,64]{1,2,0:T(8,128)}, u32[]{:S(2)}, u32[]{:S(2)}) async-start(f32[8,2048,64]{1,2,0:T(8,128)} %get-tuple-element.41), calls=%async_computation.1 | async-start | bytes 8388608 | tf_op jit(solution)/shard_map/all_to_all | solution.py:34
  338.6 4.0 %copy-start.1 = (f32[822,512]{1,0:T(8,128)S(1)}, f32[822,512]{1,0:T(8,128)}, u32[]{:S(2)}) copy-start(f32[822,512]{1,0:T(8,128)} %param.9) | copy-start | bytes 5050372
Sparse Core Ops, SparseCore 0:
  49.8 170.1 all-reduce.2
where the time goes:
time: 351 us; the launch traced here: 349 us
  waiting for transfers between devices  113 us (32%)
  blocking collectives  81.6 us (23%)
  other arithmetic  58.3 us (17%)
  local copies, waits for them, and re-layouts  46.3 us (13%)
  matrix products  22.6 us (6%)
  between operations  14.2 us (4%)
  starting transfers between devices  13.4 us (4%)
    psum x1, waiting for transfers between devices, shards(): head_vecs = lax.psum(partial_value, ('rows', 'dim'))  113 us
    unnamed x1, blocking collectives  81.6 us
    select_n x1, other arithmetic, shards(): level = jnp.take(thresholds, thr_idx)  39.7 us
    dot_general x4, matrix products, score_block(): score = jnp.dot(rows_q, ent_low.T, preferred_element_type=jnp.float32)  22.6 us
    all_to_all x2, starting transfers between devices, several_exchanges(): lax.all_to_all(slab, axis, split_axis=0, concat_axis=0, tiled=True)  13.4 us
    gather x1, local copies, waits for them, and re-layouts, pick_rows(): picked = jnp.take(table, jnp.clip(local, 0, count - 1), axis=0)  12.9 us
    unnamed x15, local copies, waits for them, and re-layouts  9.66 us
    gather x1, local copies, waits for them, and re-layouts, shards(): jnp.take(relations, rel_ids, axis=0)  8.9 us
  transfers between devices with their start and end apart: 3, of which 1 were waited for; matrix products, arithmetic and copies ran while one was open for 29% of the time, Pallas kernels for 0%

commit v1 on v0

--- a/solution.py
+++ b/solution.py
@@ -1,9 +1,19 @@
+import functools
 import jax
 import jax.numpy as jnp
 from jax import lax
 from jax.sharding import PartitionSpec as P
 
 sharpness = 2.0
+
+
+def slot_part(shard_in, shard_axis, link_axis):
+    for pp in (shard_axis, link_axis):
+        shard_in = lax.psum(shard_in, axis_name=pp)
+    return shard_in
+
+
+supply_the_masks = functools.partial(slot_part, shard_axis="rows", link_axis="dim")
 
 
 def cut_along(value, dim, length):
@@ -50,7 +60,7 @@
     serving = several_exchanges(entity_table, "dim", 2, 1, 0)
     start = (lax.axis_index("rows") * lax.axis_size("dim") + lax.axis_index("dim")) * local_rows
     partial_value = pick_rows(entity_table, head_ids, start)
-    head_vecs = lax.psum(partial_value, ("rows", "dim"))
+    head_vecs = supply_the_masks(partial_value)
     query = (head_vecs * jnp.take(relations, rel_ids, axis=0)).astype(jnp.bfloat16)
     ent_low = entity_table.astype(jnp.bfloat16)
     level = jnp.take(thresholds, thr_idx)

time: 351 us -> 420 us (1.20)
  blocking collectives: 81.6 us -> 154 us
  starting transfers between devices: 13.4 us -> 4.66 us
  waiting for transfers between devices: 113 us -> 119 us
    all_to_all x0 -> x1, blocking collectives: none -> 89.1 us  [several_exchanges(): lax.all_to_all(slab, axis, split_axis=0, concat_axis=0, tiled=True)]
    unnamed x1, blocking collectives: 81.6 us -> 64.5 us
    all_to_all x2 -> x1, starting transfers between devices: 13.4 us -> 4.58 us  [several_exchanges(): lax.all_to_all(slab, axis, split_axis=0, concat_axis=0, tiled=True)]
    psum x1 -> x2, waiting for transfers between devices: 113 us -> 119 us  [slot_part(): shard_in = lax.psum(shard_in, axis_name=pp)]
    unnamed x15 -> x13, local copies, waits for them, and re-layouts: 9.66 us -> 9.53 us
  transfers between devices with their start and end apart: 3 -> 3, of which waited for: 1 -> 2; matrix products, arithmetic and copies ran while one was open for 29% -> 19% of each run, Pallas kernels for 0% -> 0%
where the time goes in v1:
time: 420 us; the launch traced here: 419 us
  blocking collectives  154 us (37%)
  waiting for transfers between devices  119 us (28%)
  other arithmetic  60 us (14%)
  local copies, waits for them, and re-layouts  44.6 us (11%)
  matrix products  22.6 us (5%)
  between operations  14.2 us (3%)
  starting transfers between devices  4.66 us (1%)
    psum x2, waiting for transfers between devices, slot_part(): shard_in = lax.psum(shard_in, axis_name=pp)  119 us
    all_to_all x1, blocking collectives, several_exchanges(): lax.all_to_all(slab, axis, split_axis=0, concat_axis=0, tiled=True)  89.1 us
    unnamed x1, blocking collectives  64.5 us
    select_n x1, other arithmetic, shards(): level = jnp.take(thresholds, thr_idx)  39.8 us
    dot_general x4, matrix products, score_block(): score = jnp.dot(rows_q, ent_low.T, preferred_element_type=jnp.float32)  22.6 us
    gather x1, local copies, waits for them, and re-layouts, pick_rows(): picked = jnp.take(table, jnp.clip(local, 0, count - 1), axis=0)  12.9 us
    unnamed x13, local copies, waits for them, and re-layouts  9.53 us
    gather x1, local copies, waits for them, and re-layouts, shards(): jnp.take(relations, rel_ids, axis=0)  8.91 us
  transfers between devices with their start and end apart: 3, of which 2 were waited for; matrix products, arithmetic and copies ran while one was open for 19% of the time, Pallas kernels for 0%

profile of v1, /device:TPU:1, one launch (start us, length us, event | category | flops | bytes accessed | tf_op | source)
XLA Modules:
  0.0 418.8 jit_solution(5497026439710617307)
XLA Ops:
  7.2 0.8 compare_and_fusion.2
  8.1 0.7 fusion.5
  8.8 12.9 %gather_fusion = f32[2048,512]{1,0:T(8,128)} fusion(f32[4096,512]{1,0:T(8,128)} %param.8, s32[2048]{0:T(1024)S(1)} %fusion.5), kind=kCustom, calls=%fused_computation | custom fusion | bytes 8396800 | tf_op jit(solution)/shard_map/jit(_take)/gather | solution.py:52
  21.6 3.9 select_select_fusion
  25.6 8.9 %copy.12 = f32[4096,512]{0,1:T(8,128)} copy(f32[4096,512]{1,0:T(8,128)} %param.8) | data formatting | bytes 16777216 | tf_op args[0]
  34.5 6.3 %fusion.6 = (f32[8,2048,64]{1,2,0:T(8,128)S(1)}, f32[8,2048,64]{1,2,0:T(8,128)}) fusion(f32[8,4096,64]{1,2,0:T(8,128)} %bitcast.87), kind=kLoop, calls=%fused_computation.21 | loop fusion | bytes 16777216 | tf_op jit(solution)/shard_map/split | solution.py:42
  40.8 89.1 %all_to_all.10 = f32[8,2048,64]{1,2,0:T(8,128)} all-to-all(f32[8,2048,64]{1,2,0:T(8,128)S(1)} %get-tuple-element.40), channel_id=1, replica_groups=mesh['rows'=16,'dim'=8] {'dim'}, dimensions={0} | all-to-all | bytes 8388608 | tf_op jit(solution)/shard_map/all_to_all | solution.py:44
  129.8 4.6 %all-to-all-start.1 = ((f32[8,2048,64]{1,2,0:T(8,128)}), f32[8,2048,64]{1,2,0:T(8,128)}, u32[]{:S(2)}, u32[]{:S(2)}) async-start(f32[8,2048,64]{1,2,0:T(8,128)} %get-tuple-element.41), calls=%async_computation.1 | async-start | bytes 8388608 | tf_op jit(solution)/shard_map/all_to_all | solution.py:44
  134.4 0.0 all-reduce.6.cloned.1.call-start
  134.5 72.7 %all-reduce.4.cloned.1.call-done = f32[2048,512]{1,0:T(8,128)} async-done(((f32[2048,512]{1,0:T(8,128)}), f32[2048,512]{1,0:T(8,128)}) %all-reduce.4.cloned.1.call-update) | async-done | bytes 4194320 | tf_op jit(solution)/shard_map/psum | solution.py:12
  207.3 5.9 %convert_element_type.7 = bf16[4096,512]{1,0:T(8,128)(2,1)} convert(f32[4096,512]{1,0:T(8,128)} %param.8) | non-fusion elementwise | flops 2097152 | bytes 12582912 | tf_op jit(solution)/shard_map/convert_element_type | solution.py:65
  213.2 0.7 fusion.10
  213.9 0.7 fusion.8
  214.6 0.7 fusion.7
  215.3 0.7 fusion.9
  216.1 39.8 %select_select_fusion.1 = f32[2048]{0:T(1024)S(1)} fusion(s32[2048]{0:T(1024)S(1)} %copy-done.4, f32[]{:T(128)} %bitcast.7, f32[]{:T(128)} %bitcast.8, f32[]{:T(128)} %bitcast.9, f32[]{:T(128)} %bitcast.10, f32[]{:T(128)} %bitcast.11, f32[]{:T(128)} %bitcast.12, f32[]{:T(128)} %bitcast.13, f32[]{:T(128)} %bitcast.14, f32[]{:T(128)} %bitcast.15, f32[]{:T(128)} %bitcast.16, ...), kind=kLoop, calls=%fused_computation.15 | loop fusion | flops 272384 | bytes 16640 | tf_op jit(solution)/shard_map/jit(_take)/select_n | solution.py:66
  255.9 8.9 %gather_fusion.1 = f32[2048,512]{1,0:T(8,128)} fusion(f32[822,512]{1,0:T(8,128)S(1)} %copy-done, s32[2048]{0:T(1024)S(1)} %fusion.4), kind=kCustom, calls=%fused_computation.1 | custom fusion | bytes 8396800 | tf_op jit(solution)/shard_map/jit(_take)/gather | solution.py:64
  264.9 4.0 maximum_bitcast_fusion
  268.9 3.9 copy.14
  272.8 46.3 %all-reduce.6.cloned.1.call-done = f32[2048,512]{1,0:T(8,128)} async-done(((f32[2048,512]{1,0:T(8,128)}), f32[2048,512]{1,0:T(8,128)}) %all-reduce.6.cloned.1.call-update) | async-done | bytes 4194320 | tf_op jit(solution)/shard_map/psum | solution.py:12
  319.1 4.8 %multiply_convert_fusion = bf16[2048,512]{1,0:T(8,128)(2,1)} fusion(f32[2048,512]{1,0:T(8,128)} %all-reduce.6.cloned.1.call-done, f32[2048,512]{1,0:T(8,128)} %gather_fusion.1, pred[2048]{0:T(1024)(128)(4,1)S(1)} %compare_and_fusion), kind=kLoop, calls=%fused_computation.10 | loop fusion | flops 3145728 | bytes 10487808 | tf_op jit(solution)/shard_map/convert_element_type | solution.py:64
  323.9 22.9 %while.10 = (s32[]{:T(128)}, f32[4,512]{1,0:T(4,128)S(1)}, bf16[4,512,512]{2,1,0:T(8,128)(2,1)}, bf16[4096,512]{1,0:T(8,128)(2,1)}, f32[4,512]{1,0:T(4,128)S(1)}, /*index=5*/s32[]{:T(128)}, s32[]{:T(128)}) while((s32[]{:T(128)}, f32[4,512]{1,0:T(4,128)S(1)}, bf16[4,512,512]{2,1,0:T(8,128)(2,1)}, bf16[4096,512]{1,0:T(8,128)(2,1)}, ...), condition=%wide.region_4.5_spmd, body=%wide.region_2.4_spmd.sunk | while | flops 2160066560 | bytes 4735073 | solution.py:77
  323.9 5.6 %fusion.17 = f32[512]{0:T(512)S(1)} fusion(bf16[4096,512]{1,0:T(8,128)(2,1)} %get-tuple-element.156, f32[512]{0:T(512)S(1)} %bitcast.91, bf16[4,512,512]{2,1,0:T(8,128)(2,1)} %get-tuple-element.155, s32[]{:T(128)S(6)} %copy.21), kind=kOutput, calls=%fused_computation.3.clone.1 | convolution fusion | flops 2160066048 | bytes 4722692 | tf_op jit(solution)/shard_map/while/body/eval_jaxpr/dot_general | solution.py:73
  329.6 0.1 dynamic_update_slice.5
  329.7 5.6 %fusion.17 = f32[512]{0:T(512)S(1)} fusion(bf16[4096,512]{1,0:T(8,128)(2,1)} %get-tuple-element.156, f32[512]{0:T(512)S(1)} %bitcast.91, bf16[4,512,512]{2,1,0:T(8,128)(2,1)} %get-tuple-element.155, s32[]{:T(128)S(6)} %copy.21), kind=kOutput, calls=%fused_computation.3.clone.1 | convolution fusion | flops 2160066048 | bytes 4722692 | tf_op jit(solution)/shard_map/while/body/eval_jaxpr/dot_general | solution.py:73
  335.3 0.1 dynamic_update_slice.5
  335.4 5.6 %fusion.17 = f32[512]{0:T(512)S(1)} fusion(bf16[4096,512]{1,0:T(8,128)(2,1)} %get-tuple-element.156, f32[512]{0:T(512)S(1)} %bitcast.91, bf16[4,512,512]{2,1,0:T(8,128)(2,1)} %get-tuple-element.155, s32[]{:T(128)S(6)} %copy.21), kind=kOutput, calls=%fused_computation.3.clone.1 | convolution fusion | flops 2160066048 | bytes 4722692 | tf_op jit(solution)/shard_map/while/body/eval_jaxpr/dot_general | solution.py:73
  341.0 0.1 dynamic_update_slice.5
  341.1 5.6 %fusion.17 = f32[512]{0:T(512)S(1)} fusion(bf16[4096,512]{1,0:T(8,128)(2,1)} %get-tuple-element.156, f32[512]{0:T(512)S(1)} %bitcast.91, bf16[4,512,512]{2,1,0:T(8,128)(2,1)} %get-tuple-element.155, s32[]{:T(128)S(6)} %copy.21), kind=kOutput, calls=%fused_computation.3.clone.1 | convolution fusion | flops 2160066048 | bytes 4722692 | tf_op jit(solution)/shard_map/while/body/eval_jaxpr/dot_general | solution.py:73
  346.8 0.1 dynamic_update_slice.5
  346.9 64.5 %all-reduce = f32[2048]{0:T(1024)S(1)} all-reduce(f32[2048]{0:T(1024)S(1)} %bitcast.92), channel_id=2, replica_groups=mesh['rows'=16,'dim'=8] {'rows','dim'}, use_global_device_ids=true, to_apply=%region_5.6.clone | all-reduce | flops 2048 | bytes 16384
  411.3 0.6 dynamic-slice
  (27 shorter events, 0.2 us)
Async XLA Ops:
  7.2 248.8 %copy-start = (f32[822,512]{1,0:T(8,128)S(1)}, f32[822,512]{1,0:T(8,128)}, u32[]{:S(2)}) copy-start(f32[822,512]{1,0:T(8,128)} %param.9) | copy-start | bytes 5050372
  7.2 200.0 %all-reduce.4.cloned.1.call-start = ((), (), s32[]{:S(2)}) async-start(), calls=%async_computation.2 | async-start | bytes 8388608 | tf_op jit(solution)/shard_map/psum | solution.py:12
  129.8 135.0 %all-to-all-start.1 = ((f32[8,2048,64]{1,2,0:T(8,128)}), f32[8,2048,64]{1,2,0:T(8,128)}, u32[]{:S(2)}, u32[]{:S(2)}) async-start(f32[8,2048,64]{1,2,0:T(8,128)} %get-tuple-element.41), calls=%async_computation.1 | async-start | bytes 8388608 | tf_op jit(solution)/shard_map/all_to_all | solution.py:44
  134.4 184.7 %all-reduce.6.cloned.1.call-start = ((), (), s32[]{:S(2)}) async-start(), calls=%async_computation.3 | async-start | bytes 8388608 | tf_op jit(solution)/shard_map/psum | solution.py:12
  207.2 6.0 %copy-start.2 = (f32[64]{0:T(128)S(1)}, f32[64]{0:T(128)}, u32[]{:S(2)}) copy-start(f32[64]{0:T(128)} %param.10) | copy-start | bytes 772
  207.3 8.8 %copy-start.4 = (s32[2048]{0:T(1024)S(1)}, s32[2048]{0:T(1024)}, u32[]{:S(2)}) copy-start(s32[2048]{0:T(1024)} %param.13) | copy-start | bytes 24580
  207.3 48.6 %copy-start.3 = (s32[2048]{0:T(1024)S(1)}, s32[2048]{0:T(1024)}, u32[]{:S(2)}) copy-start(s32[2048]{0:T(1024)} %param.12) | copy-start | bytes 24580
  346.8 65.1 %copy-start.1 = (f32[822,512]{1,0:T(8,128)S(1)}, f32[822,512]{1,0:T(8,128)}, u32[]{:S(2)}) copy-start(f32[822,512]{1,0:T(8,128)} %param.9) | copy-start | bytes 5050372
Sparse Core Ops, SparseCore 0:
  25.7 181.4 all-reduce.3
  209.7 109.3 all-reduce.5
